TPU v7x, 128 devices: a whole 4x4x4 slice. The times are simulated.
128 devices in a mesh: rep: 1, dp: 128 (over x, y, z, core).
Axes of the slice: x: 4, y: 4, z: 4, core: 2. Of those that a mesh axis runs over, the one named last changes fastest.
Arguments:
- x: bfloat16 [128, 1024, 1280], P(('rep', 'dp'))
- dy: bfloat16 [128, 1024, 1280], P(('rep', 'dp'))
- w_gate: bfloat16 [2, 1280, 4096], replicated
- w_up: bfloat16 [2, 1280, 4096], replicated
- w_down: bfloat16 [2, 4096, 1280], replicated
- m_w_gate: float32 [2, 1280, 4096], P(None, 'dp')
- m_w_up: float32 [2, 1280, 4096], P(None, 'dp')
- m_w_down: float32 [2, 4096, 1280], P(None, 'dp')
- v_w_gate: float32 [2, 1280, 4096], P(None, 'dp')
- v_w_up: float32 [2, 1280, 4096], P(None, 'dp')
- v_w_down: float32 [2, 4096, 1280], P(None, 'dp')
Outputs:
- output 1: bfloat16 [2, 1280, 4096], P('rep')
- output 2: bfloat16 [2, 1280, 4096], P('rep')
- output 3: bfloat16 [2, 4096, 1280], P('rep')
- output 4: float32 [2, 1280, 4096], P('rep', 'dp')
- output 5: float32 [2, 1280, 4096], P('rep', 'dp')
- output 6: float32 [2, 4096, 1280], P('rep', 'dp')
- output 7: float32 [2, 1280, 4096], P('rep', 'dp')
- output 8: float32 [2, 1280, 4096], P('rep', 'dp')
- output 9: float32 [2, 4096, 1280], P('rep', 'dp')
All inputs are finite; a program needn't handle non-finite values.
Results may differ from a plain program's by a relative error of at most 0.022.
Values are sent between devices in bfloat16 or wider.
A program may use at most 1.5 GiB of HBM per device.

v0:
```python
import functools

import jax
import jax.numpy as jnp
from jax import lax
from jax.experimental import pallas as pl
from jax.experimental.pallas import tpu as pltpu
from jax.sharding import PartitionSpec as P

MESH = pl.DeviceIdType.MESH
BF = jnp.bfloat16
F32 = jnp.float32


KINDS = ("zyx", "xzy", "yxz")


def neighbour(axis, by):
    me = lax.axis_index("dp")
    here = {"x": me // 32, "y": me // 8 % 4, "z": me // 2 % 4, "c": me % 2}
    size = 2 if axis == "c" else 4
    here[axis] = lax.rem(here[axis] + by, size)
    return {"dp": ((here["x"] * 4 + here["y"]) * 4 + here["z"]) * 2 + here["c"]}


PEERS = [(a, by) for a in "xyz" for by in (1, 2, 3)] + [("c", 1)]


def greet():
    barrier = pltpu.get_barrier_semaphore()
    for axis, by in PEERS:
        pl.semaphore_signal(barrier, inc=1, device_id=neighbour(axis, by), device_id_type=MESH)
    pl.semaphore_wait(barrier, len(PEERS))


def gather_kernel(own_g, own_u, own_d, out_g, out_u, out_d, local_sem, send_sem, recv_sem):
    me = lax.axis_index("dp")
    here = {"x": me // 32, "y": me // 8 % 4, "z": me // 2 % 4}
    c = me % 2
    greet()
    owns, outs = (own_g, own_u, own_d), (out_g, out_u, out_d)
    started = []

    def view(k, **where):
        spots = [where.get(a, slice(None)) for a in "xyz"]
        return outs[k].at[(slice(None), *spots, c)]

    def push(src, dst, axis, by):
        n = len(started)
        copy = pltpu.make_async_remote_copy(
            src_ref=src, dst_ref=dst, send_sem=send_sem.at[n], recv_sem=recv_sem.at[n], device_id=neighbour(axis, by), device_id_type=MESH
        )
        copy.start()
        started.append(copy)
        return copy

    first, second, third, relay, swaps = {}, {}, {}, {}, []
    keep = []
    for k in range(3):
        local = pltpu.make_async_copy(owns[k], view(k, **here), local_sem.at[k])
        local.start()
        keep.append(local)
        first[k] = [push(owns[k], view(k, **here), KINDS[k][0], by) for by in (1, 3, 2)]
    for k, (a, b, e) in enumerate(KINDS):
        keep[k].wait()
        for copy in first[k]:
            copy.wait_recv()
        line = view(k, **{b: here[b], e: here[e]})
        second[k] = [push(line, line, b, by) for by in (1, 3, 2)]
    for k, (a, b, e) in enumerate(KINDS):
        for copy in second[k]:
            copy.wait_recv()
        plane = view(k, **{e: here[e]})
        third[k] = [push(plane, plane, e, by) for by in (1, 3)]
        swaps.append(push(plane, plane, "c", 1))
    for k, (a, b, e) in enumerate(KINDS):
        relay[k] = []
        for copy, by, half in zip(third[k], (1, 3), (slice(0, 2), slice(2, 4))):
            copy.wait_recv()
            came = lax.rem(here[e] + 4 - by, 4)
            part = view(k, **{e: came, a: half})
            relay[k].append(push(part, part, e, by))
            plane = view(k, **{e: came})
            swaps.append(push(plane, plane, "c", 1))
    for k, (a, b, e) in enumerate(KINDS):
        for copy, half in zip(relay[k], (slice(0, 2), slice(2, 4))):
            copy.wait_recv()
            part = view(k, **{e: lax.rem(here[e] + 2, 4), a: half})
            swaps.append(push(part, part, "c", 1))
    for copy in swaps:
        copy.wait_recv()
    for copy in started:
        copy.wait_send()


COPIES = 3 * (3 + 3 + 2 + 2 + 5)


def gather(owns):
    shapes = [jax.ShapeDtypeStruct((2, 4, 4, 4, 2, *o.shape[1:]), o.dtype) for o in owns]
    return pl.pallas_call(
        gather_kernel,
        out_shape=shapes,
        in_specs=[pl.BlockSpec(memory_space=pltpu.VMEM)] * 3,
        out_specs=[pl.BlockSpec(memory_space=pl.ANY)] * 3,
        scratch_shapes=[pltpu.SemaphoreType.DMA((3,)), pltpu.SemaphoreType.DMA((COPIES,)), pltpu.SemaphoreType.DMA((COPIES,))],
        compiler_params=pltpu.CompilerParams(collective_id=0, has_side_effects=True),
        name="gather",
    )(*owns)


def place():
    me = lax.axis_index("dp")
    return me // 32, me // 8 % 4, me // 2 % 4, me % 2


def combine(dst, terms):
    *lead, rows, _ = dst.shape
    strips = rows // 16
    count = strips
    for n in lead:
        count *= n

    @pl.loop(0, count)
    def _(i):
        spot, q = [], i // strips
        for n in reversed(lead):
            spot.insert(0, q % n)
            q = q // n
        where = (*spot, pl.ds(pl.multiple_of(i % strips * 16, 16), 16), slice(None))
        out = terms[0][where].astype(F32)
        for t in terms[1:]:
            out = out + t[where].astype(F32)
        dst[where] = out.astype(dst.dtype)


def transposed_product(a, b, out, rows, columns):
    depth = a.shape[0]

    def tile(a_ref, b_ref, o_ref):
        o_ref[...] = lax.dot_general(a_ref[...], b_ref[...], (((0,), (0,)), ((), ())), preferred_element_type=F32).astype(BF)

    pltpu.emit_pipeline(
        tile,
        grid=(a.shape[1] // rows, b.shape[1] // columns),
        in_specs=[pl.BlockSpec((depth, rows), lambda i, j: (0, i)), pl.BlockSpec((depth, columns), lambda i, j: (0, j))],
        out_specs=[pl.BlockSpec((rows, columns), lambda i, j: (i, j))],
    )(a, b, out)


STEPS = (0, 1, 2)
BYS = (1, 3, 2)


def scatter_kernel(beside, g_g, g_u, g_d, *rest):
    ins, rest = rest[: 2 * beside], rest[2 * beside :]
    f_g, f_u, f_d = rest[:3]
    products, rest = rest[3 : 3 + beside], rest[3 + beside :]
    o_g, r_g, p_g, q_g, o_u, r_u, p_u, q_u, o_d, r_d, p_d, q_d, t_d, local_sem, send_sem, recv_sem = rest
    px, py, pz, pc = place()
    greet()
    started = []

    def push(src, dst, axis, by):
        n = len(started)
        copy = pltpu.make_async_remote_copy(
            src_ref=src, dst_ref=dst, send_sem=send_sem.at[n], recv_sem=recv_sem.at[n], device_id=neighbour(axis, by), device_id_type=MESH
        )
        copy.start()
        started.append(copy)
        return copy

    def half(k, c):
        if k == 2:
            return g_d.at[:, :, :, c]
        return (g_g, g_u)[k].at[:, :, :, pl.ds(pl.multiple_of(c * 2048, 2048), 2048)]

    own, swapped = (o_g, o_u, o_d), (r_g, r_u, r_d)
    firsts, seconds = (p_g, p_u, p_d), (q_g, q_u, q_d)
    axes = ("xy", "yx", "zx")
    here = {"x": px, "y": py, "z": pz}

    def first_part(k, ref, t):
        return (ref.at[t], ref.at[:, t], ref.at[:, :, t])[k]

    def second_part(k, ref, t):
        return (ref.at[px, t], ref.at[t, py], ref.at[t, :, pz])[k]

    swaps, loads = [], []
    for k in range(3):
        swaps.append(push(half(k, 1 - pc), swapped[k], "c", 1))
        loads.append(pltpu.make_async_copy(half(k, pc), own[k], local_sem.at[k]))
        loads[k].start()

    def product(n):
        if n < beside:
            transposed_product(ins[2 * n], ins[2 * n + 1], products[n], *((512, 1280) if n == 0 else (640, 1024)))

    ring = {}
    for k in range(3):
        loads[k].wait()
        swaps[k].wait_recv()
        ring[k] = []
        for i, by in enumerate(BYS):
            t = lax.rem(here[axes[k][0]] + by, 4)
            part = first_part(k, own[k], t)
            combine(part, [part, first_part(k, swapped[k], t)])
            ring[k].append(push(part, firsts[k].at[i], axes[k][0], by))
    for n in STEPS:
        product(n)
    ring2 = {}
    for k in range(3):
        for copy in ring[k]:
            copy.wait_recv()
        ring2[k] = []
        for i, by in enumerate(BYS):
            t = lax.rem(here[axes[k][1]] + by, 4)
            part = second_part(k, own[k], t)
            combine(part, [part, second_part(k, swapped[k], t)] + [firsts[k].at[s, t] for s in STEPS])
            ring2[k].append(push(part, seconds[k].at[i], axes[k][1], by))
    last = []
    for copy in ring2[2]:
        copy.wait_recv()

    def terms_d(u):
        return [o_d.at[px, u, pz], r_d.at[px, u, pz]] + [p_d.at[s, px, u] for s in STEPS] + [q_d.at[s, u] for s in STEPS]

    for i, by in enumerate(BYS):
        u = lax.rem(py + by, 4)
        combine(o_d.at[px, u, pz], terms_d(u))
        last.append(push(o_d.at[px, u, pz], t_d.at[i], "y", by))
    for k, f in ((0, f_g), (1, f_u)):
        for copy in ring2[k]:
            copy.wait_recv()
        t = here[axes[k][1]]
        combine(f, [second_part(k, own[k], t), second_part(k, swapped[k], t)] + [firsts[k].at[s, t] for s in STEPS] + [seconds[k].at[s] for s in STEPS])
    for copy in last:
        copy.wait_recv()
    combine(f_d, terms_d(py) + [t_d.at[s] for s in STEPS])
    for copy in started:
        copy.wait_send()


def scatter(g_g, g_u, g_d, beside, identity):
    any_space, vmem = pl.BlockSpec(memory_space=pl.ANY), pl.BlockSpec(memory_space=pltpu.VMEM)
    copies = 3 + 9 + 9 + 3
    wide, tall = (4, 80, 2048), (4, 32, 1280)
    shapes = []
    for _ in range(2):
        shapes += [(4, *wide), (4, *wide), (3, *wide), (3, *wide[1:])]
    shapes += [(4, 4, *tall), (4, 4, *tall), (3, 4, *tall), (3, *tall), (3, *tall[1:])]
    operands = [t for pair in beside for t in pair]
    out = pl.pallas_call(
        functools.partial(scatter_kernel, len(beside)),
        out_shape=[jax.ShapeDtypeStruct((80, 2048), F32)] * 2
        + [jax.ShapeDtypeStruct((32, 1280), F32)]
        + [jax.ShapeDtypeStruct((a.shape[1], b.shape[1]), BF) for a, b in beside],
        in_specs=[any_space] * (3 + len(operands)),
        out_specs=[vmem] * 3 + [any_space] * len(beside),
        scratch_shapes=[pltpu.VMEM(s, BF) for s in shapes]
        + [pltpu.SemaphoreType.DMA((3,)), pltpu.SemaphoreType.DMA((copies,)), pltpu.SemaphoreType.DMA((copies,))],
        compiler_params=pltpu.CompilerParams(collective_id=identity, has_side_effects=True, vmem_limit_bytes=66_000_000),
        name=f"scatter{identity}",
    )(g_g.reshape(4, 4, 80, 4096), g_u.reshape(4, 4, 80, 4096), g_d.reshape(4, 4, 4, 2, 32, 1280), *operands)
    return out[:3], out[3:]


COLUMN = [(dz, dc) for dz in range(4) for dc in range(2) if dz or dc]


def column_kernel(parts, kept, out, came, send_sem, recv_sem):
    px, py, pz, pc = place()

    def peer(dz, dc):
        return {"dp": ((px * 4 + py) * 4 + lax.rem(pz + dz, 4)) * 2 + lax.rem(pc + dc, 2)}

    barrier = pltpu.get_barrier_semaphore()
    for dz, dc in COLUMN:
        pl.semaphore_signal(barrier, inc=1, device_id=peer(dz, dc), device_id_type=MESH)
    pl.semaphore_wait(barrier, len(COLUMN))
    copies = []
    for n, (dz, dc) in enumerate(COLUMN):
        copy = pltpu.make_async_remote_copy(
            src_ref=parts.at[lax.rem(pz + dz, 4), lax.rem(pc + dc, 2)],
            dst_ref=came.at[pz, pc],
            send_sem=send_sem.at[n],
            recv_sem=recv_sem.at[n],
            device_id=peer(dz, dc),
            device_id_type=MESH,
        )
        copy.start()
        copies.append(copy)
    for copy in copies:
        copy.wait_recv()
    other = 1 - pc
    for w in range(out.shape[1]):
        mine = kept[w]
        for by in (1, 2, 3):
            mine = mine + came[lax.rem(pz + by, 4), pc, w].astype(F32)
        out[pc, w] = mine
        theirs = came[0, other, w].astype(F32)
        for z in (1, 2, 3):
            theirs = theirs + came[z, other, w].astype(F32)
        out[other, w] = theirs
    for copy in copies:
        copy.wait_send()


def column(sums, pz, pc):
    n = len(sums)
    blocks = jnp.stack([s.reshape(4, 2, 10, 16, 128) for s in sums], 2)
    kept = lax.dynamic_slice(blocks, (pz, pc, 0, 0, 0, 0), (1, 1, n, 10, 16, 128))[0, 0]
    vmem = pl.BlockSpec(memory_space=pltpu.VMEM)
    out = pl.pallas_call(
        column_kernel,
        out_shape=jax.ShapeDtypeStruct((2, n, 10, 16, 128), F32),
        in_specs=[vmem] * 2,
        out_specs=vmem,
        scratch_shapes=[pltpu.VMEM((4, 2, n, 10, 16, 128), BF), pltpu.SemaphoreType.DMA((7,)), pltpu.SemaphoreType.DMA((7,))],
        compiler_params=pltpu.CompilerParams(collective_id=3, has_side_effects=True),
        name="column",
    )(blocks.astype(BF), kept)
    return [out[:, w].transpose(1, 0, 2, 3).reshape(10, 4096) for w in range(n)]


def adamw(w, m, v, g):
    m = 0.9 * m + 0.1 * g
    v = 0.95 * v + 0.05 * g * g
    step = m * lax.rsqrt(v + 1e-8) + 0.1 * w
    return (w - 0.02 * step).astype(BF), m, v


def matmul(a, w):
    return jnp.dot(a, w, preferred_element_type=F32).astype(BF)


def normed(h):
    wide = h.astype(F32)
    scale = lax.rsqrt(jnp.mean(wide**2, -1, keepdims=True) + 1e-6)
    return (wide * scale).astype(BF)


def forward(h, wg, wu, wd):
    a = normed(h)
    gate = jnp.dot(a, wg, preferred_element_type=F32)
    up = jnp.dot(a, wu, preferred_element_type=F32)
    act = (jax.nn.silu(gate) * up).astype(BF)
    out = None if wd is None else h + matmul(act, wd)
    return out, (a, gate, up, act)


def across(a, w):
    return lax.dot_general(a, w, (((1,), (1,)), ((), ())), preferred_element_type=F32).astype(BF)


def product_of(a, b):
    return lax.dot_general(a, b, (((0,), (0,)), ((), ())), preferred_element_type=F32).astype(BF)


def backward(h, kept, by_out, wg, wu, wd, through):
    a, gate, up, act = kept
    by_act = across(by_out, wd).astype(F32)
    sig = jax.nn.sigmoid(gate)
    by_up = (by_act * (gate * sig)).astype(BF)
    by_gate = (by_act * up * (sig * (1 + gate * (1 - sig)))).astype(BF)
    pairs = [(a, by_gate), (a, by_up), (act, by_out)]
    if not through:
        return pairs, None
    by_a = across(by_gate, wg).astype(F32) + across(by_up, wu).astype(F32)
    _, back = jax.vjp(normed, h)
    return pairs, by_out + back(by_a.astype(BF))[0]


BESIDE = True


def solution(mesh):
    def body(x, dy, wg, wu, wd, mg, mu, md, vg, vu, vd):
        me = lax.axis_index("dp")
        px, py, pz, pc = place()
        h0, by_y = x[0], dy[0]
        h1, kept0 = forward(h0, wg[0], wu[0], wd[0])
        _, kept1 = forward(h1, wg[1], wu[1], None)
        pairs1, by_h1 = backward(h1, kept1, by_y, wg[1], wu[1], wd[1], True)
        pairs0, _ = backward(h0, kept0, by_h1, wg[0], wu[0], wd[0], False)
        by_1 = [product_of(*pair) for pair in pairs1]
        if BESIDE:
            sums1, by_0 = scatter(*by_1, [pairs0[2], pairs0[0], pairs0[1]], 1)
            by_0 = (by_0[1], by_0[2], by_0[0])
        else:
            sums1, _ = scatter(*by_1, [], 1)
            by_0 = [product_of(*pair) for pair in pairs0]
        sums0, _ = scatter(*by_0, [], 2)
        wide = column([sums0[0], sums1[0], sums0[1], sums1[1]], pz, pc)
        sums = {(0, 0): wide[0], (0, 1): wide[1], (1, 0): wide[2], (1, 1): wide[3], (2, 0): sums0[2], (2, 1): sums1[2]}
        new = {}
        for (i, n), g in sums.items():
            rows = g.shape[0]
            own = lax.dynamic_slice_in_dim((wg, wu, wd)[i][n], me * rows, rows, 0).astype(F32)
            new[i, n] = adamw(own, (mg, mu, md)[i][n], (vg, vu, vd)[i][n], g.astype(BF).astype(F32))
        stacked = [[jnp.stack([new[i, n][which] for n in range(2)]) for i in range(3)] for which in range(3)]
        owns = [stacked[0][0].reshape(2, 320, 128), stacked[0][1].reshape(2, 320, 128), stacked[0][2]]
        weights = [o.reshape(w.shape) for o, w in zip(gather(owns), (wg, wu, wd))]
        return (*weights, *stacked[1], *stacked[2])

    rows = P(None, "dp", None)
    return jax.shard_map(
        body,
        mesh=mesh,
        in_specs=(P("dp"), P("dp"), P(), P(), P(), *[rows] * 6),
        out_specs=(P(), P(), P(), *[rows] * 6),
        check_vma=False,
    )
```

profile of v0, /device:TPU:1, one launch (start us, length us, event | category | flops | bytes accessed | tf_op | source)
XLA Modules:
  0.0 778.1 jit_solution(12755218483480578219)
XLA Ops:
  0.6 2.3 fusion.32
  3.0 18.1 %fusion.24 = f32[1024,4096]{1,0:T(8,128)} fusion(bf16[1,1024,1280]{2,1,0:T(8,128)(2,1)} %param.11, f32[1024]{0:T(1024)S(1)} %add_rsqrt_fusion, bf16[2,1280,4096]{2,1,0:T(8,128)(2,1)} %param.13), kind=kOutput, calls=%fused_computation.35 | convolution fusion | flops 10741350400 | bytes 29888512 | tf_op jit(solution)/shard_map/dot_general | solution.py:345
  21.1 22.3 %multiply_convert_fusion.1 = (bf16[1024,4096]{1,0:T(8,128)(2,1)S(1)}, f32[1024,4096]{1,0:T(8,128)}) fusion(f32[1024,4096]{1,0:T(8,128)} %fusion.24, bf16[2,1280,4096]{2,1,0:T(8,128)(2,1)} %param.14, bf16[1,1024,1280]{2,1,0:T(8,128)(2,1)S(1)} %copy-done.1, f32[1024]{0:T(1024)S(1)} %add_rsqrt_fusion), kind=kOutput, calls=%fused_computation.13 | convolution fusion | flops 10766516224 | bytes 55054336 | tf_op jit(solution)/shard_map/dot_general | solution.py:346
  43.4 18.5 %fusion.36 = (f32[1024]{0:T(1024)S(1)}, bf16[1024,1280]{1,0:T(8,128)(2,1)S(1)}) fusion(bf16[1024,4096]{1,0:T(8,128)(2,1)S(1)} %get-tuple-element.82.rest_0_, bf16[2,4096,1280]{2,1,0:T(8,128)(2,1)} %param.15, bf16[1,1024,1280]{2,1,0:T(8,128)(2,1)S(1)} %copy-done.1), kind=kOutput, calls=%fused_computation.50 | convolution fusion | flops 10743970816 | bytes 24121344 | tf_op jit(solution)/shard_map/dot_general | solution.py:334
  61.9 18.0 %fusion.14 = f32[1024,4096]{1,0:T(8,128)} fusion(bf16[1024,1280]{1,0:T(8,128)(2,1)S(1)} %get-tuple-element.85, f32[1024]{0:T(1024)S(1)} %fusion.96, bf16[2,1280,4096]{2,1,0:T(8,128)(2,1)} %param.14), kind=kOutput, calls=%fused_computation.25 | convolution fusion | flops 10741350400 | bytes 29888512 | tf_op jit(solution)/shard_map/dot_general | solution.py:346
  80.0 17.4 %fusion.10 = f32[1024,4096]{1,0:T(8,128)} fusion(bf16[1024,1280]{1,0:T(8,128)(2,1)S(1)} %get-tuple-element.85, f32[1024]{0:T(1024)S(1)} %fusion.96, bf16[2,1280,4096]{2,1,0:T(8,128)(2,1)} %param.13), kind=kOutput, calls=%fused_computation.21 | convolution fusion | flops 10741350400 | bytes 29888512 | tf_op jit(solution)/shard_map/dot_general | solution.py:345
  97.3 25.2 %fusion.2 = (bf16[1024,4096]{1,0:T(8,128)(2,1)}, bf16[1024,4096]{1,0:T(8,128)(2,1)}) fusion(f32[1024,4096]{1,0:T(8,128)} %fusion.10, f32[1024,4096]{1,0:T(8,128)} %fusion.14, bf16[2,4096,1280]{2,1,0:T(8,128)(2,1)} %param.15, bf16[1,1024,1280]{2,1,0:T(8,128)(2,1)S(1)} %copy-done.4), kind=kOutput, calls=%fused_computation.6 | convolution fusion | flops 10800332800 | bytes 63438848 | tf_op jit(solution)/shard_map/dot_general | solution.py:353
  122.6 18.0 %fusion.42 = bf16[1024,1280]{1,0:T(8,128)(2,1)} fusion(bf16[1024,4096]{1,0:T(8,128)(2,1)} %get-tuple-element.56, bf16[2,1280,4096]{2,1,0:T(8,128)(2,1)} %param.14), kind=kOutput, calls=%fused_computation.56 | convolution fusion | flops 10738728960 | bytes 21495808 | tf_op jit(solution)/shard_map/dot_general | solution.py:353
  140.6 18.3 %fusion.38 = (f32[1024]{0:T(1024)S(1)}, bf16[1024,1280]{1,0:T(8,128)(2,1)}) fusion(bf16[1024,1280]{1,0:T(8,128)(2,1)S(1)} %copy-done.6, bf16[1024,1280]{1,0:T(8,128)(2,1)} %fusion.42, bf16[1024,4096]{1,0:T(8,128)(2,1)} %get-tuple-element.57, bf16[2,1280,4096]{2,1,0:T(8,128)(2,1)} %param.13), kind=kOutput, calls=%fused_computation.52 | convolution fusion | flops 10749213696 | bytes 26742784 | tf_op jit(solution)/shard_map/dot_general | solution.py:353
  158.9 4.0 fusion.55.rest_1_
  163.0 26.1 %fusion.5 = (bf16[1024,4096]{1,0:T(8,128)(2,1)}, bf16[1024,4096]{1,0:T(8,128)(2,1)}) fusion(f32[1024,4096]{1,0:T(8,128)} %fusion.24, f32[1024,4096]{1,0:T(8,128)} %get-tuple-element.83, bf16[1024,1280]{1,0:T(8,128)(2,1)S(1)} %fusion.55.rest_1_, bf16[2,4096,1280]{2,1,0:T(8,128)(2,1)} %param.15), kind=kOutput, calls=%fused_computation.9 | convolution fusion | flops 10800332800 | bytes 63438848 | tf_op jit(solution)/shard_map/dot_general | solution.py:353
  189.0 17.9 %convolution_convert_fusion.1 = bf16[1280,4096]{1,0:T(8,128)(2,1)} fusion(bf16[1024,4096]{1,0:T(8,128)(2,1)} %get-tuple-element.56, bf16[1024,1280]{1,0:T(8,128)(2,1)} %copy-done.5, f32[1024]{0:T(1024)S(1)} %fusion.96), kind=kOutput, calls=%fused_computation.17 | convolution fusion | flops 10746593280 | bytes 21499904 | tf_op jit(solution)/shard_map/dot_general | solution.py:357
  206.9 17.1 %convolution_convert_fusion.2 = bf16[1280,4096]{1,0:T(8,128)(2,1)} fusion(bf16[1024,4096]{1,0:T(8,128)(2,1)} %get-tuple-element.57, bf16[1024,1280]{1,0:T(8,128)(2,1)S(1)} %copy-done.7, f32[1024]{0:T(1024)S(1)} %fusion.96), kind=kOutput, calls=%fused_computation.18 | convolution fusion | flops 10746593280 | bytes 21499904 | tf_op jit(solution)/shard_map/dot_general | solution.py:357
  224.0 21.2 %convolution_convert_fusion = bf16[4096,1280]{1,0:T(8,128)(2,1)} fusion(f32[1024,4096]{1,0:T(8,128)} %fusion.14, f32[1024,4096]{1,0:T(8,128)} %fusion.10, bf16[1,1024,1280]{2,1,0:T(8,128)(2,1)} %param.12), kind=kOutput, calls=%fused_computation.16 | convolution fusion | flops 10767826944 | bytes 46661632 | tf_op jit(solution)/shard_map/dot_general | solution.py:357
  245.2 2.0 fusion.33.rest_2_.rest_4_
  247.2 126.8 %scatter1.1 = (f32[80,2048]{1,0:T(8,128)}, f32[80,2048]{1,0:T(8,128)}, f32[32,1280]{1,0:T(8,128)}, bf16[4096,1280]{1,0:T(8,128)(2,1)}, bf16[1280,4096]{1,0:T(8,128)(2,1)}, /*index=5*/bf16[1280,4096]{1,0:T(8,128)(2,1)}) custom-call(bf16[4,4,80,4096]{3,2,1,0:T(8,128)(2,1)} %bitcast.192, bf16[4,4,80,4096]{3,2,1,0:T(8,128)(2,1)} %bitcast.191, ...), custom_call_target="tpu_custom_call" | custom-call | tf_op jit(solution)/shard_map/scatter1/pallas_call | solution.py:253
  374.0 117.6 %scatter2.1 = (f32[80,2048]{1,0:T(8,128)}, f32[80,2048]{1,0:T(8,128)}, f32[32,1280]{1,0:T(8,128)}) custom-call(bf16[4,4,80,4096]{3,2,1,0:T(8,128)(2,1)} %bitcast.189, bf16[4,4,80,4096]{3,2,1,0:T(8,128)(2,1)} %bitcast.190, bf16[4,4,4,2,32,1280]{5,4,3,2,1,0:T(8,128)(2,1)} %bitcast.188), custom_call_target="tpu_custom_call" | custom-call | tf_op jit(solution)/shard_map/scatter2/pallas_call | solution.py:253
  491.6 1.2 copy.48
  492.8 1.2 copy.49
  494.1 1.2 copy.50
  496.4 1.2 convert_element_type.338.parts
  497.6 21.0 %column.1 = f32[2,4,10,16,128]{4,3,2,1,0:T(8,128)} custom-call(bf16[4,2,4,10,16,128]{5,4,3,2,1,0:T(8,128)(2,1)} %convert_element_type.338.parts, f32[4,10,16,128]{3,2,1,0:T(8,128)} %dynamic-slice_bitcast_fusion.kept), custom_call_target="tpu_custom_call" | custom-call | tf_op jit(solution)/shard_map/column/pallas_call | solution.py:314
  518.6 1.1 convert.20
  520.0 8.5 %fusion.120 = (bf16[1,1280,4096]{2,1,0:T(8,128)(2,1)S(1)}, bf16[1,1280,4096]{2,1,0:T(8,128)(2,1)S(1)}) fusion(bf16[2,1280,4096]{2,1,0:T(8,128)(2,1)} %param.14), kind=kLoop, calls=%fused_computation.164 | loop fusion | bytes 41943040 | tf_op jit(solution)/shard_map/slice | solution.py:382
  529.9 1.0 copy.39
  531.0 8.5 %fusion.121 = (bf16[1,1280,4096]{2,1,0:T(8,128)(2,1)S(1)}, bf16[1,1280,4096]{2,1,0:T(8,128)(2,1)S(1)}) fusion(bf16[2,1280,4096]{2,1,0:T(8,128)(2,1)} %param.13), kind=kLoop, calls=%fused_computation.165 | loop fusion | bytes 41943040 | tf_op jit(solution)/shard_map/slice | solution.py:399
  541.0 1.0 copy.38
  542.0 8.3 %fusion.119 = (bf16[1,4096,1280]{2,1,0:T(8,128)(2,1)S(1)}, bf16[1,4096,1280]{2,1,0:T(8,128)(2,1)S(1)}) fusion(bf16[2,4096,1280]{2,1,0:T(8,128)(2,1)} %param.15), kind=kLoop, calls=%fused_computation.163 | loop fusion | bytes 41943040 | tf_op jit(solution)/shard_map/slice | solution.py:382
  555.7 142.4 %gather.1 = (bf16[2,4,4,4,2,320,128]{6,5,4,3,2,1,0:T(8,128)(2,1)}, bf16[2,4,4,4,2,320,128]{6,5,4,3,2,1,0:T(8,128)(2,1)}, bf16[2,4,4,4,2,32,1280]{6,5,4,3,2,1,0:T(8,128)(2,1)}) custom-call(bf16[2,320,128]{2,1,0:T(8,128)(2,1)} %pad_maximum_fusion.6.own_g, bf16[2,320,128]{2,1,0:T(8,128)(2,1)} %pad_maximum_fusion.7.own_u, ...), custom_call_target="tpu_custom_call" | custom-call | tf_op jit(solution)/shard_map/gather/pallas_call | solution.py:101
  698.1 31.2 %reshape.251 = bf16[2,1280,4096]{2,1,0:T(8,128)(2,1)} reshape(bf16[2,4,4,4,2,320,128]{6,5,4,3,2,1,0:T(8,128)(2,1)} %get-tuple-element.30) | data formatting | bytes 41943040 | tf_op jit(solution)/shard_map/reshape | solution.py:403
  729.3 31.2 %reshape.252 = bf16[2,1280,4096]{2,1,0:T(8,128)(2,1)} reshape(bf16[2,4,4,4,2,320,128]{6,5,4,3,2,1,0:T(8,128)(2,1)} %get-tuple-element.31) | data formatting | bytes 41943040 | tf_op jit(solution)/shard_map/reshape | solution.py:403
  760.6 17.1 %copy.88 = bf16[2,4096,1280]{2,1,0:T(8,128)(2,1)} copy(bf16[2,4096,1280]{2,1,0:T(8,128)(2,1)} %bitcast.187) | data formatting | bytes 41943040
  (81 shorter events, 9.6 us)
Async XLA Ops:
  3.0 18.1 %copy-start.19 = (f32[1024]{0:T(1024)}, f32[1024]{0:T(1024)S(1)}, u32[]{:S(2)}) copy-start(f32[1024]{0:T(1024)S(1)} %add_rsqrt_fusion) | copy-start | bytes 12292
  3.0 18.1 %copy-start.1 = (bf16[1,1024,1280]{2,1,0:T(8,128)(2,1)S(1)}, bf16[1,1024,1280]{2,1,0:T(8,128)(2,1)}, u32[]{:S(2)}) copy-start(bf16[1,1024,1280]{2,1,0:T(8,128)(2,1)} %param.11) | copy-start | bytes 7864324
  43.4 18.5 %copy-start.3 = (bf16[1024,4096]{1,0:T(8,128)(2,1)}, bf16[1024,4096]{1,0:T(8,128)(2,1)S(1)}, u32[]{:S(2)}) copy-start(bf16[1024,4096]{1,0:T(8,128)(2,1)S(1)} %get-tuple-element.82.rest_0_) | copy-start | bytes 25165828
  61.9 18.1 %copy-start.5 = (bf16[1024,1280]{1,0:T(8,128)(2,1)}, bf16[1024,1280]{1,0:T(8,128)(2,1)S(1)}, u32[]{:S(2)}) copy-start(bf16[1024,1280]{1,0:T(8,128)(2,1)S(1)} %get-tuple-element.85) | copy-start | bytes 7864324
  61.9 18.1 %copy-start.17 = (f32[1024]{0:T(1024)}, f32[1024]{0:T(1024)S(1)}, u32[]{:S(2)}) copy-start(f32[1024]{0:T(1024)S(1)} %get-tuple-element.84) | copy-start | bytes 12292
  80.0 17.4 %copy-start.4 = (bf16[1,1024,1280]{2,1,0:T(8,128)(2,1)S(1)}, bf16[1,1024,1280]{2,1,0:T(8,128)(2,1)}, u32[]{:S(2)}) copy-start(bf16[1,1024,1280]{2,1,0:T(8,128)(2,1)} %param.12) | copy-start | bytes 7864324
  122.6 18.1 %copy-start.6 = (bf16[1024,1280]{1,0:T(8,128)(2,1)S(1)}, bf16[1024,1280]{1,0:T(8,128)(2,1)}, u32[]{:S(2)}) copy-start(bf16[1024,1280]{1,0:T(8,128)(2,1)} %copy-done.5) | copy-start | bytes 7864324
  140.6 18.3 %copy-start.18 = (f32[1024]{0:T(1024)S(1)}, f32[1024]{0:T(1024)}, u32[]{:S(2)}) copy-start(f32[1024]{0:T(1024)} %copy-done.17) | copy-start | bytes 12292
  163.0 26.1 %copy-start = (bf16[1024,1280]{1,0:T(8,128)(2,1)}, bf16[1024,1280]{1,0:T(8,128)(2,1)S(1)}, u32[]{:S(2)}) copy-start(bf16[1024,1280]{1,0:T(8,128)(2,1)S(1)} %fusion.55.rest_1_) | copy-start | bytes 7864324
  189.0 17.9 %copy-start.7 = (bf16[1024,1280]{1,0:T(8,128)(2,1)S(1)}, bf16[1024,1280]{1,0:T(8,128)(2,1)}, u32[]{:S(2)}) copy-start(bf16[1024,1280]{1,0:T(8,128)(2,1)} %copy-done.5) | copy-start | bytes 7864324
  224.0 21.2 %copy-start.2 = (bf16[1,1024,1280]{2,1,0:T(8,128)(2,1)S(1)}, bf16[1,1024,1280]{2,1,0:T(8,128)(2,1)}, u32[]{:S(2)}) copy-start(bf16[1,1024,1280]{2,1,0:T(8,128)(2,1)} %param.11) | copy-start | bytes 7864324
  224.0 21.2 %copy-start.20 = (f32[1024]{0:T(1024)S(1)}, f32[1024]{0:T(1024)}, u32[]{:S(2)}) copy-start(f32[1024]{0:T(1024)} %copy-done.19) | copy-start | bytes 12292
  374.0 121.4 %copy-start.8 = (f32[80,2048]{1,0:T(8,128)S(1)}, f32[80,2048]{1,0:T(8,128)}, u32[]{:S(2)}) copy-start(f32[80,2048]{1,0:T(8,128)} %get-tuple-element.27) | copy-start | bytes 1966084
  519.9 8.5 %copy-start.9 = (f32[2,10,4096]{2,0,1:T(2,128)S(1)}, f32[2,10,4096]{2,0,1:T(2,128)}, u32[]{:S(2)}) copy-start(f32[2,10,4096]{2,0,1:T(2,128)} %param.17) | copy-start | bytes 983044
  519.9 8.9 %copy-start.10 = (f32[2,10,4096]{2,0,1:T(2,128)S(1)}, f32[2,10,4096]{2,0,1:T(2,128)}, u32[]{:S(2)}) copy-start(f32[2,10,4096]{2,0,1:T(2,128)} %param.20) | copy-start | bytes 983044
  531.0 8.5 %copy-start.11 = (f32[2,10,4096]{2,0,1:T(2,128)S(1)}, f32[2,10,4096]{2,0,1:T(2,128)}, u32[]{:S(2)}) copy-start(f32[2,10,4096]{2,0,1:T(2,128)} %param.16) | copy-start | bytes 983044
  531.0 8.9 %copy-start.12 = (f32[2,10,4096]{2,0,1:T(2,128)S(1)}, f32[2,10,4096]{2,0,1:T(2,128)}, u32[]{:S(2)}) copy-start(f32[2,10,4096]{2,0,1:T(2,128)} %param.19) | copy-start | bytes 983044
  541.9 8.3 %copy-start.13 = (f32[2,32,1280]{2,1,0:T(8,128)S(1)}, f32[2,32,1280]{2,1,0:T(8,128)}, u32[]{:S(2)}) copy-start(f32[2,32,1280]{2,1,0:T(8,128)} %param.21) | copy-start | bytes 983044
  542.0 8.3 %copy-start.14 = (f32[2,32,1280]{2,1,0:T(8,128)S(1)}, f32[2,32,1280]{2,1,0:T(8,128)}, u32[]{:S(2)}) copy-start(f32[2,32,1280]{2,1,0:T(8,128)} %param.18) | copy-start | bytes 983044
  542.0 8.3 %copy-start.15 = (f32[32,1280]{1,0:T(8,128)S(1)}, f32[32,1280]{1,0:T(8,128)}, u32[]{:S(2)}) copy-start(f32[32,1280]{1,0:T(8,128)} %get-tuple-element.29) | copy-start | bytes 491524
  542.0 8.3 %copy-start.16 = (f32[32,1280]{1,0:T(8,128)S(1)}, f32[32,1280]{1,0:T(8,128)}, u32[]{:S(2)}) copy-start(f32[32,1280]{1,0:T(8,128)} %get-tuple-element.28) | copy-start | bytes 491524
where the time goes:
time: 789 us; the launch traced here: 778 us
  Pallas kernels  408 us (52%)
  matrix products  238 us (30%)
  local copies, waits for them, and re-layouts  115 us (15%)
  other arithmetic  15.5 us (2%)
    pallas_call x2, Pallas kernels, scatter(): pl.pallas_call(functools.partial(scatter_kernel, len(beside)), out_shape=...  244 us
    pallas_call x1, Pallas kernels, gather(): pl.pallas_call(gather_kernel, out_shape=shapes, in_specs=[pl.BlockSpec(me...  142 us
    dot_general x4, matrix products, across(): lax.dot_general(a, w, (((1,), (1,)), ((), ())), preferred_element_type=F32)  87.7 us
    reshape x2, local copies, waits for them, and re-layouts, body(): weights = [o.reshape(w.shape) for o, w in zip(gather(owns), (wg, wu, wd))]  62.4 us
    dot_general x3, matrix products, product_of(): lax.dot_general(a, b, (((0,), (0,)), ((), ())), preferred_element_type=F32)  56.1 us
    dot_general x2, matrix products, forward(): up = jnp.dot(a, wu, preferred_element_type=F32)  40.3 us
    dot_general x2, matrix products, forward(): gate = jnp.dot(a, wg, preferred_element_type=F32)  35.5 us
    unnamed x54, local copies, waits for them, and re-layouts  25 us

commit v1 on v0

--- a/solution.py
+++ b/solution.py
@@ -149,6 +149,7 @@
 
 
 STEPS = (0, 1, 2)
+SIDES = (0, 1)
 BYS = (1, 3, 2)
 
 
@@ -170,11 +171,6 @@
         started.append(copy)
         return copy
 
-    def half(k, c):
-        if k == 2:
-            return g_d.at[:, :, :, c]
-        return (g_g, g_u)[k].at[:, :, :, pl.ds(pl.multiple_of(c * 2048, 2048), 2048)]
-
     own, swapped = (o_g, o_u, o_d), (r_g, r_u, r_d)
     firsts, seconds = (p_g, p_u, p_d), (q_g, q_u, q_d)
     axes = ("xy", "yx", "zx")
@@ -186,28 +182,54 @@
     def second_part(k, ref, t):
         return (ref.at[px, t], ref.at[t, py], ref.at[t, :, pz])[k]
 
-    swaps, loads = [], []
-    for k in range(3):
-        swaps.append(push(half(k, 1 - pc), swapped[k], "c", 1))
-        loads.append(pltpu.make_async_copy(half(k, pc), own[k], local_sem.at[k]))
-        loads[k].start()
+    def chunk(k, c, t):
+        if k == 2:
+            return g_d.at[:, :, t, c]
+        lanes = pl.ds(pl.multiple_of(c * 2048, 2048), 2048)
+        return g_g.at[t, :, :, lanes] if k == 0 else g_u.at[:, t, :, lanes]
+
+    swaps, loads = {}, {}
+    for i, by in enumerate((2, 1, 3, 0)):
+        for k in range(3):
+            t = lax.rem(here[axes[k][0]] + by, 4)
+            swaps[k, by] = push(chunk(k, 1 - pc, t), first_part(k, swapped[k], t), "c", 1)
+            loads[k, by] = pltpu.make_async_copy(chunk(k, pc, t), first_part(k, own[k], t), local_sem.at[i * 3 + k])
+            loads[k, by].start()
 
     def product(n):
         if n < beside:
             transposed_product(ins[2 * n], ins[2 * n + 1], products[n], *((512, 1280) if n == 0 else (640, 1024)))
 
-    ring = {}
-    for k in range(3):
-        loads[k].wait()
-        swaps[k].wait_recv()
-        ring[k] = []
-        for i, by in enumerate(BYS):
-            t = lax.rem(here[axes[k][0]] + by, 4)
-            part = first_part(k, own[k], t)
-            combine(part, [part, first_part(k, swapped[k], t)])
-            ring[k].append(push(part, firsts[k].at[i], axes[k][0], by))
-    for n in STEPS:
-        product(n)
+    low, high = pl.ds(0, 2), pl.ds(2, 2)
+
+    def part_of(k, ref, by, side):
+        t = lax.rem(here[axes[k][0]] + by, 4)
+        return (ref.at[t, side], ref.at[side, t], ref.at[side, :, t])[k]
+
+    def add_and_push(k, by, side, more, slot, towards):
+        part = part_of(k, own[k], by, side)
+        combine(part, [part, part_of(k, swapped[k], by, side)] + more)
+        return push(part, firsts[k].at[slot, side], axes[k][0], towards)
+
+    relays, ring = {}, {k: [] for k in range(3)}
+    for k in range(3):
+        loads[k, 2].wait()
+        swaps[k, 2].wait_recv()
+        relays[k] = (add_and_push(k, 2, low, [], 2, 1), add_and_push(k, 2, high, [], 2, 3))
+    for k in range(3):
+        for by, side, slot in ((1, high, 0), (3, low, 1)):
+            loads[k, by].wait()
+            swaps[k, by].wait_recv()
+            ring[k].append(add_and_push(k, by, side, [], slot, by))
+    product(0)
+    for k in range(3):
+        for copy, by, side, slot in zip(relays[k], (1, 3), (low, high), (0, 1)):
+            copy.wait_recv()
+            ring[k].append(add_and_push(k, by, side, [firsts[k].at[2, side]], slot, by))
+    product(1)
+    for k in range(3):
+        loads[k, 0].wait()
+        swaps[k, 0].wait_recv()
     ring2 = {}
     for k in range(3):
         for copy in ring[k]:
@@ -216,14 +238,15 @@
         for i, by in enumerate(BYS):
             t = lax.rem(here[axes[k][1]] + by, 4)
             part = second_part(k, own[k], t)
-            combine(part, [part, second_part(k, swapped[k], t)] + [firsts[k].at[s, t] for s in STEPS])
+            combine(part, [part, second_part(k, swapped[k], t)] + [firsts[k].at[s, t] for s in SIDES])
             ring2[k].append(push(part, seconds[k].at[i], axes[k][1], by))
+    product(2)
     last = []
     for copy in ring2[2]:
         copy.wait_recv()
 
     def terms_d(u):
-        return [o_d.at[px, u, pz], r_d.at[px, u, pz]] + [p_d.at[s, px, u] for s in STEPS] + [q_d.at[s, u] for s in STEPS]
+        return [o_d.at[px, u, pz], r_d.at[px, u, pz]] + [p_d.at[s, px, u] for s in SIDES] + [q_d.at[s, u] for s in STEPS]
 
     for i, by in enumerate(BYS):
         u = lax.rem(py + by, 4)
@@ -233,7 +256,7 @@
         for copy in ring2[k]:
             copy.wait_recv()
         t = here[axes[k][1]]
-        combine(f, [second_part(k, own[k], t), second_part(k, swapped[k], t)] + [firsts[k].at[s, t] for s in STEPS] + [seconds[k].at[s] for s in STEPS])
+        combine(f, [second_part(k, own[k], t), second_part(k, swapped[k], t)] + [firsts[k].at[s, t] for s in SIDES] + [seconds[k].at[s] for s in STEPS])
     for copy in last:
         copy.wait_recv()
     combine(f_d, terms_d(py) + [t_d.at[s] for s in STEPS])
@@ -243,7 +266,7 @@
 
 def scatter(g_g, g_u, g_d, beside, identity):
     any_space, vmem = pl.BlockSpec(memory_space=pl.ANY), pl.BlockSpec(memory_space=pltpu.VMEM)
-    copies = 3 + 9 + 9 + 3
+    copies = 12 + 18 + 9 + 3
     wide, tall = (4, 80, 2048), (4, 32, 1280)
     shapes = []
     for _ in range(2):
@@ -258,7 +281,7 @@
         in_specs=[any_space] * (3 + len(operands)),
         out_specs=[vmem] * 3 + [any_space] * len(beside),
         scratch_shapes=[pltpu.VMEM(s, BF) for s in shapes]
-        + [pltpu.SemaphoreType.DMA((3,)), pltpu.SemaphoreType.DMA((copies,)), pltpu.SemaphoreType.DMA((copies,))],
+        + [pltpu.SemaphoreType.DMA((12,)), pltpu.SemaphoreType.DMA((copies,)), pltpu.SemaphoreType.DMA((copies,))],
         compiler_params=pltpu.CompilerParams(collective_id=identity, has_side_effects=True, vmem_limit_bytes=66_000_000),
         name=f"scatter{identity}",
     )(g_g.reshape(4, 4, 80, 4096), g_u.reshape(4, 4, 80, 4096), g_d.reshape(4, 4, 4, 2, 32, 1280), *operands)
@@ -392,13 +415,13 @@
             by_0 = [product_of(*pair) for pair in pairs0]
         sums0, _ = scatter(*by_0, [], 2)
         wide = column([sums0[0], sums1[0], sums0[1], sums1[1]], pz, pc)
-        sums = {(0, 0): wide[0], (0, 1): wide[1], (1, 0): wide[2], (1, 1): wide[3], (2, 0): sums0[2], (2, 1): sums1[2]}
-        new = {}
-        for (i, n), g in sums.items():
-            rows = g.shape[0]
-            own = lax.dynamic_slice_in_dim((wg, wu, wd)[i][n], me * rows, rows, 0).astype(F32)
-            new[i, n] = adamw(own, (mg, mu, md)[i][n], (vg, vu, vd)[i][n], g.astype(BF).astype(F32))
-        stacked = [[jnp.stack([new[i, n][which] for n in range(2)]) for i in range(3)] for which in range(3)]
+        sums = [jnp.stack(wide[:2]), jnp.stack(wide[2:]), jnp.stack([sums0[2], sums1[2]])]
+        new = []
+        for g, w, m, v in zip(sums, (wg, wu, wd), (mg, mu, md), (vg, vu, vd)):
+            rows = g.shape[1]
+            own = lax.dynamic_slice(w, (0, me * rows, 0), (2, rows, w.shape[2])).astype(F32)
+            new.append(adamw(own, m, v, g.astype(BF).astype(F32)))
+        stacked = [[t[which] for t in new] for which in range(3)]
         owns = [stacked[0][0].reshape(2, 320, 128), stacked[0][1].reshape(2, 320, 128), stacked[0][2]]
         weights = [o.reshape(w.shape) for o, w in zip(gather(owns), (wg, wu, wd))]
         return (*weights, *stacked[1], *stacked[2])

time: 789 us -> 718 us (0.910)
  Pallas kernels: 408 us -> 359 us
  local copies, waits for them, and re-layouts: 115 us -> 90.1 us
    pallas_call x2, Pallas kernels: 244 us -> 195 us  [scatter(): pl.pallas_call(functools.partial(scatter_kernel, len(beside)), out_shape=...]
    slice x7 -> x0, local copies, waits for them, and re-layouts: 26.6 us -> none  [the longest x2 16.8 us: body(): h1, kept0 = forward(h0, wg[0], wu[0], wd[0])]
    unnamed x54 -> x36, local copies, waits for them, and re-layouts: 25 us -> 25 us
where the time goes in v1:
time: 718 us; the launch traced here: 707 us
  Pallas kernels  359 us (50%)
  matrix products  238 us (33%)
  local copies, waits for them, and re-layouts  90.1 us (13%)
  other arithmetic  18.3 us (3%)
    pallas_call x2, Pallas kernels, scatter(): pl.pallas_call(functools.partial(scatter_kernel, len(beside)), out_shape=...  195 us
    pallas_call x1, Pallas kernels, gather(): pl.pallas_call(gather_kernel, out_shape=shapes, in_specs=[pl.BlockSpec(me...  142 us
    dot_general x4, matrix products, across(): lax.dot_general(a, w, (((1,), (1,)), ((), ())), preferred_element_type=F32)  87.3 us
    reshape x2, local copies, waits for them, and re-layouts, body(): weights = [o.reshape(w.shape) for o, w in zip(gather(owns), (wg, wu, wd))]  62.4 us
    dot_general x3, matrix products, product_of(): lax.dot_general(a, b, (((0,), (0,)), ((), ())), preferred_element_type=F32)  55.4 us
    dot_general x2, matrix products, forward(): up = jnp.dot(a, wu, preferred_element_type=F32)  39.4 us
    dot_general x2, matrix products, forward(): gate = jnp.dot(a, wg, preferred_element_type=F32)  37.4 us
    unnamed x36, local copies, waits for them, and re-layouts  25 us

profile of v1, /device:TPU:1, one launch (start us, length us, event | category | flops | bytes accessed | tf_op | source)
XLA Modules:
  0.0 706.9 jit_solution(16252500763048378819)
XLA Ops:
  0.7 2.3 fusion.41
  3.0 3.8 fusion.42.rest_2_.rest_4_
  6.8 19.3 %fusion.24 = f32[1024,4096]{1,0:T(8,128)} fusion(bf16[2,1280,4096]{2,1,0:T(8,128)(2,1)} %param.13, bf16[1,1024,1280]{2,1,0:T(8,128)(2,1)} %param.11, f32[1024]{0:T(1024)S(1)} %add_rsqrt_fusion), kind=kOutput, calls=%fused_computation.35 | convolution fusion | flops 10741350400 | bytes 29888512 | tf_op jit(solution)/shard_map/dot_general | solution.py:368
  26.1 22.2 %multiply_convert_fusion.1 = (bf16[1024,4096]{1,0:T(8,128)(2,1)S(1)}, f32[1024,4096]{1,0:T(8,128)}) fusion(f32[1024,4096]{1,0:T(8,128)} %fusion.24, bf16[2,1280,4096]{2,1,0:T(8,128)(2,1)} %param.14, bf16[1,1024,1280]{2,1,0:T(8,128)(2,1)S(1)} %copy-done.1, f32[1024]{0:T(1024)S(1)} %add_rsqrt_fusion), kind=kOutput, calls=%fused_computation.13 | convolution fusion | flops 10766516224 | bytes 55054336 | tf_op jit(solution)/shard_map/dot_general | solution.py:369
  48.3 18.5 %fusion.45 = (f32[1024]{0:T(1024)S(1)}, bf16[1024,1280]{1,0:T(8,128)(2,1)S(1)}) fusion(bf16[1024,4096]{1,0:T(8,128)(2,1)S(1)} %get-tuple-element.59.rest_0_, bf16[2,4096,1280]{2,1,0:T(8,128)(2,1)} %param.15, bf16[1,1024,1280]{2,1,0:T(8,128)(2,1)S(1)} %copy-done.1), kind=kOutput, calls=%fused_computation.59 | convolution fusion | flops 10743970816 | bytes 24121344 | tf_op jit(solution)/shard_map/dot_general | solution.py:357
  66.8 18.1 %fusion.10 = f32[1024,4096]{1,0:T(8,128)} fusion(bf16[2,1280,4096]{2,1,0:T(8,128)(2,1)} %param.13, bf16[1024,1280]{1,0:T(8,128)(2,1)S(1)} %get-tuple-element.62, f32[1024]{0:T(1024)S(1)} %fusion.84), kind=kOutput, calls=%fused_computation.21 | convolution fusion | flops 10741350400 | bytes 29888512 | tf_op jit(solution)/shard_map/dot_general | solution.py:368
  85.0 17.2 %fusion.14 = f32[1024,4096]{1,0:T(8,128)} fusion(bf16[2,1280,4096]{2,1,0:T(8,128)(2,1)} %param.14, bf16[1024,1280]{1,0:T(8,128)(2,1)S(1)} %get-tuple-element.62, f32[1024]{0:T(1024)S(1)} %fusion.84), kind=kOutput, calls=%fused_computation.25 | convolution fusion | flops 10741350400 | bytes 29888512 | tf_op jit(solution)/shard_map/dot_general | solution.py:369
  102.2 20.5 %convolution_convert_fusion = bf16[4096,1280]{1,0:T(8,128)(2,1)} fusion(f32[1024,4096]{1,0:T(8,128)} %fusion.14, f32[1024,4096]{1,0:T(8,128)} %fusion.10, bf16[1,1024,1280]{2,1,0:T(8,128)(2,1)S(1)} %copy-done.3), kind=kOutput, calls=%fused_computation.16 | convolution fusion | flops 10767826944 | bytes 46661632 | tf_op jit(solution)/shard_map/dot_general | solution.py:380
  122.7 25.1 %fusion.2 = (bf16[1024,4096]{1,0:T(8,128)(2,1)}, bf16[1024,4096]{1,0:T(8,128)(2,1)}) fusion(f32[1024,4096]{1,0:T(8,128)} %fusion.10, f32[1024,4096]{1,0:T(8,128)} %fusion.14, bf16[2,4096,1280]{2,1,0:T(8,128)(2,1)} %param.15, bf16[1,1024,1280]{2,1,0:T(8,128)(2,1)S(1)} %copy-done.3), kind=kOutput, calls=%fused_computation.6 | convolution fusion | flops 10800332800 | bytes 63438848 | tf_op jit(solution)/shard_map/dot_general | solution.py:376
  147.8 17.7 %fusion.51 = bf16[1024,1280]{1,0:T(8,128)(2,1)} fusion(bf16[1024,4096]{1,0:T(8,128)(2,1)} %get-tuple-element.53, bf16[2,1280,4096]{2,1,0:T(8,128)(2,1)} %param.14), kind=kOutput, calls=%fused_computation.65 | convolution fusion | flops 10738728960 | bytes 21495808 | tf_op jit(solution)/shard_map/dot_general | solution.py:376
  165.5 18.3 %fusion.47 = (f32[1024]{0:T(1024)S(1)}, bf16[1024,1280]{1,0:T(8,128)(2,1)}) fusion(bf16[1024,1280]{1,0:T(8,128)(2,1)S(1)} %copy-done.5, bf16[1024,1280]{1,0:T(8,128)(2,1)} %fusion.51, bf16[1024,4096]{1,0:T(8,128)(2,1)} %get-tuple-element.54, bf16[2,1280,4096]{2,1,0:T(8,128)(2,1)} %param.13), kind=kOutput, calls=%fused_computation.61 | convolution fusion | flops 10749213696 | bytes 26742784 | tf_op jit(solution)/shard_map/dot_general | solution.py:376
  183.9 4.0 fusion.64.rest_1_
  187.9 26.1 %fusion.5 = (bf16[1024,4096]{1,0:T(8,128)(2,1)}, bf16[1024,4096]{1,0:T(8,128)(2,1)}) fusion(f32[1024,4096]{1,0:T(8,128)} %fusion.24, f32[1024,4096]{1,0:T(8,128)} %get-tuple-element.60, bf16[1024,1280]{1,0:T(8,128)(2,1)S(1)} %fusion.64.rest_1_, bf16[2,4096,1280]{2,1,0:T(8,128)(2,1)} %param.15), kind=kOutput, calls=%fused_computation.9 | convolution fusion | flops 10800332800 | bytes 63438848 | tf_op jit(solution)/shard_map/dot_general | solution.py:376
  214.0 17.9 %convolution_convert_fusion.2 = bf16[1280,4096]{1,0:T(8,128)(2,1)} fusion(bf16[1024,4096]{1,0:T(8,128)(2,1)} %get-tuple-element.54, bf16[1024,1280]{1,0:T(8,128)(2,1)} %copy-done.4, f32[1024]{0:T(1024)S(1)} %fusion.84), kind=kOutput, calls=%fused_computation.18 | convolution fusion | flops 10746593280 | bytes 21499904 | tf_op jit(solution)/shard_map/dot_general | solution.py:380
  231.9 17.1 %convolution_convert_fusion.1 = bf16[1280,4096]{1,0:T(8,128)(2,1)} fusion(bf16[1024,4096]{1,0:T(8,128)(2,1)} %get-tuple-element.53, bf16[1024,1280]{1,0:T(8,128)(2,1)S(1)} %copy-done.6, f32[1024]{0:T(1024)S(1)} %fusion.84), kind=kOutput, calls=%fused_computation.17 | convolution fusion | flops 10746593280 | bytes 21499904 | tf_op jit(solution)/shard_map/dot_general | solution.py:380
  248.9 103.9 %scatter1.1 = (f32[80,2048]{1,0:T(8,128)}, f32[80,2048]{1,0:T(8,128)}, f32[32,1280]{1,0:T(8,128)}, bf16[4096,1280]{1,0:T(8,128)(2,1)}, bf16[1280,4096]{1,0:T(8,128)(2,1)}, /*index=5*/bf16[1280,4096]{1,0:T(8,128)(2,1)}) custom-call(bf16[4,4,80,4096]{3,2,1,0:T(8,128)(2,1)} %bitcast.130, bf16[4,4,80,4096]{3,2,1,0:T(8,128)(2,1)} %bitcast.131, ...), custom_call_target="tpu_custom_call" | custom-call | tf_op jit(solution)/shard_map/scatter1/pallas_call | solution.py:276
  352.8 90.8 %scatter2.1 = (f32[80,2048]{1,0:T(8,128)}, f32[80,2048]{1,0:T(8,128)}, f32[32,1280]{1,0:T(8,128)}) custom-call(bf16[4,4,80,4096]{3,2,1,0:T(8,128)(2,1)} %bitcast.127, bf16[4,4,80,4096]{3,2,1,0:T(8,128)(2,1)} %bitcast.128, bf16[4,4,4,2,32,1280]{5,4,3,2,1,0:T(8,128)(2,1)} %bitcast.126), custom_call_target="tpu_custom_call" | custom-call | tf_op jit(solution)/shard_map/scatter2/pallas_call | solution.py:276
  443.6 1.2 copy.36
  444.8 1.2 copy.38
  446.0 1.0 convert_bitcast_fusion
  447.1 2.0 fusion.81
  449.1 1.2 copy.37
  451.4 1.3 convert_element_type.146.parts
  452.7 22.1 %column.1 = f32[2,4,10,16,128]{4,3,2,1,0:T(8,128)} custom-call(bf16[4,2,4,10,16,128]{5,4,3,2,1,0:T(8,128)(2,1)} %convert_element_type.146.parts, f32[4,10,16,128]{3,2,1,0:T(8,128)} %dynamic-slice_bitcast_fusion.kept), custom_call_target="tpu_custom_call" | custom-call | tf_op jit(solution)/shard_map/column/pallas_call | solution.py:337
  474.8 1.1 convert.30
  476.3 2.7 fusion.71
  480.5 1.0 copy.34
  482.5 1.0 copy.35
  484.5 142.3 %gather.1 = (bf16[2,4,4,4,2,320,128]{6,5,4,3,2,1,0:T(8,128)(2,1)}, bf16[2,4,4,4,2,320,128]{6,5,4,3,2,1,0:T(8,128)(2,1)}, bf16[2,4,4,4,2,32,1280]{6,5,4,3,2,1,0:T(8,128)(2,1)}) custom-call(bf16[2,320,128]{2,1,0:T(8,128)(2,1)} %reshape.97.own_g, bf16[2,320,128]{2,1,0:T(8,128)(2,1)} %reshape.98.own_u, bf16[2,32,1280]{2,1,0:T(8,128)(2,1)} %get-tuple-element.42.own_d), custom_call_target="tpu_custom_call" | custom-call | tf_op jit(solution)/shard_map/gather/pallas_call | solution.py:101
  626.8 31.2 %reshape.99 = bf16[2,1280,4096]{2,1,0:T(8,128)(2,1)} reshape(bf16[2,4,4,4,2,320,128]{6,5,4,3,2,1,0:T(8,128)(2,1)} %get-tuple-element.30) | data formatting | bytes 41943040 | tf_op jit(solution)/shard_map/reshape | solution.py:426
  658.0 31.2 %reshape.100 = bf16[2,1280,4096]{2,1,0:T(8,128)(2,1)} reshape(bf16[2,4,4,4,2,320,128]{6,5,4,3,2,1,0:T(8,128)(2,1)} %get-tuple-element.31) | data formatting | bytes 41943040 | tf_op jit(solution)/shard_map/reshape | solution.py:426
  689.2 17.1 %copy.60 = bf16[2,4096,1280]{2,1,0:T(8,128)(2,1)} copy(bf16[2,4096,1280]{2,1,0:T(8,128)(2,1)} %bitcast.125) | data formatting | bytes 41943040
  (46 shorter events, 4.9 us)
Async XLA Ops:
  6.8 19.3 %copy-start.1 = (bf16[1,1024,1280]{2,1,0:T(8,128)(2,1)S(1)}, bf16[1,1024,1280]{2,1,0:T(8,128)(2,1)}, u32[]{:S(2)}) copy-start(bf16[1,1024,1280]{2,1,0:T(8,128)(2,1)} %param.11) | copy-start | bytes 7864324
  48.3 18.5 %copy-start.2 = (bf16[1024,4096]{1,0:T(8,128)(2,1)}, bf16[1024,4096]{1,0:T(8,128)(2,1)S(1)}, u32[]{:S(2)}) copy-start(bf16[1024,4096]{1,0:T(8,128)(2,1)S(1)} %get-tuple-element.59.rest_0_) | copy-start | bytes 25165828
  66.8 18.2 %copy-start.4 = (bf16[1024,1280]{1,0:T(8,128)(2,1)}, bf16[1024,1280]{1,0:T(8,128)(2,1)S(1)}, u32[]{:S(2)}) copy-start(bf16[1024,1280]{1,0:T(8,128)(2,1)S(1)} %get-tuple-element.62) | copy-start | bytes 7864324
  66.8 18.2 %copy-start.10 = (f32[1024]{0:T(1024)}, f32[1024]{0:T(1024)S(1)}, u32[]{:S(2)}) copy-start(f32[1024]{0:T(1024)S(1)} %get-tuple-element.61) | copy-start | bytes 12292
  85.0 17.2 %copy-start.3 = (bf16[1,1024,1280]{2,1,0:T(8,128)(2,1)S(1)}, bf16[1,1024,1280]{2,1,0:T(8,128)(2,1)}, u32[]{:S(2)}) copy-start(bf16[1,1024,1280]{2,1,0:T(8,128)(2,1)} %param.12) | copy-start | bytes 7864324
  147.8 17.7 %copy-start.5 = (bf16[1024,1280]{1,0:T(8,128)(2,1)S(1)}, bf16[1024,1280]{1,0:T(8,128)(2,1)}, u32[]{:S(2)}) copy-start(bf16[1024,1280]{1,0:T(8,128)(2,1)} %copy-done.4) | copy-start | bytes 7864324
  165.5 18.3 %copy-start.11 = (f32[1024]{0:T(1024)S(1)}, f32[1024]{0:T(1024)}, u32[]{:S(2)}) copy-start(f32[1024]{0:T(1024)} %copy-done.10) | copy-start | bytes 12292
  187.9 26.1 %copy-start = (bf16[1024,1280]{1,0:T(8,128)(2,1)}, bf16[1024,1280]{1,0:T(8,128)(2,1)S(1)}, u32[]{:S(2)}) copy-start(bf16[1024,1280]{1,0:T(8,128)(2,1)S(1)} %fusion.64.rest_1_) | copy-start | bytes 7864324
  214.0 17.9 %copy-start.6 = (bf16[1024,1280]{1,0:T(8,128)(2,1)S(1)}, bf16[1024,1280]{1,0:T(8,128)(2,1)}, u32[]{:S(2)}) copy-start(bf16[1024,1280]{1,0:T(8,128)(2,1)} %copy-done.4) | copy-start | bytes 7864324
  352.8 94.2 %copy-start.9 = (f32[2,32,1280]{2,1,0:T(8,128)S(1)}, f32[2,32,1280]{2,1,0:T(8,128)}, u32[]{:S(2)}) copy-start(f32[2,32,1280]{2,1,0:T(8,128)} %param.21) | copy-start | bytes 983044
  352.8 97.5 %copy-start.7 = (f32[80,2048]{1,0:T(8,128)S(1)}, f32[80,2048]{1,0:T(8,128)}, u32[]{:S(2)}) copy-start(f32[80,2048]{1,0:T(8,128)} %get-tuple-element.27) | copy-start | bytes 1966084
  450.3 26.0 %copy-start.8 = (f32[2,10,4096]{2,0,1:T(2,128)S(1)}, f32[2,10,4096]{2,0,1:T(2,128)}, u32[]{:S(2)}) copy-start(f32[2,10,4096]{2,0,1:T(2,128)} %param.19) | copy-start | bytes 983044

commit v2 on v1

--- a/solution.py
+++ b/solution.py
@@ -26,24 +26,33 @@
 PEERS = [(a, by) for a in "xyz" for by in (1, 2, 3)] + [("c", 1)]
 
 
-def greet():
+def across_column(dz, dc):
+    px, py, pz, pc = place()
+    return {"dp": ((px * 4 + py) * 4 + lax.rem(pz + dz, 4)) * 2 + lax.rem(pc + dc, 2)}
+
+
+def greet(more=()):
     barrier = pltpu.get_barrier_semaphore()
-    for axis, by in PEERS:
-        pl.semaphore_signal(barrier, inc=1, device_id=neighbour(axis, by), device_id_type=MESH)
-    pl.semaphore_wait(barrier, len(PEERS))
-
-
-def gather_kernel(own_g, own_u, own_d, out_g, out_u, out_d, local_sem, send_sem, recv_sem):
-    me = lax.axis_index("dp")
-    here = {"x": me // 32, "y": me // 8 % 4, "z": me // 2 % 4}
-    c = me % 2
-    greet()
-    owns, outs = (own_g, own_u, own_d), (out_g, out_u, out_d)
+    for device in [neighbour(axis, by) for axis, by in PEERS] + list(more):
+        pl.semaphore_signal(barrier, inc=1, device_id=device, device_id_type=MESH)
+    pl.semaphore_wait(barrier, len(PEERS) + len(more))
+
+
+def gather_kernel(own_g, own_u, own_d, out_g, out_u, out_d, came_g, came_u, tall, wide_g, wide_u, local_sem, send_sem, recv_sem, column_send, column_recv):
+    px, py, pz, c = place()
+    here = {"x": px, "y": py, "z": pz}
+    greet([across_column(dz, 1) for dz in (1, 2, 3)])
+    owns, outs = (wide_g, wide_u, own_d), (out_g, out_u, out_d)
     started = []
 
     def view(k, **where):
-        spots = [where.get(a, slice(None)) for a in "xyz"]
-        return outs[k].at[(slice(None), *spots, c)]
+        x, y, z = (where.get(a, slice(None)) for a in "xyz")
+        if k == 2:
+            return outs[k].at[:, x, y, z, c]
+        first, count = c * 2048, 2048
+        if "z" in where:
+            first, count = (c * 2048 + z.start * 512, 1024) if isinstance(z, slice) else (c * 2048 + z * 512, 512)
+        return outs[k].at[:, x, y, :, pl.ds(pl.multiple_of(first, 512), count)]
 
     def push(src, dst, axis, by):
         n = len(started)
@@ -54,12 +63,33 @@
         started.append(copy)
         return copy
 
+    column_copies = []
+    for k, (own, came) in enumerate(((own_g, came_g), (own_u, came_u))):
+        for n, (dz, dc) in enumerate(COLUMN):
+            copy = pltpu.make_async_remote_copy(
+                src_ref=own.at[lax.rem(pz + dz, 4), lax.rem(c + dc, 2)],
+                dst_ref=came.at[pz, c],
+                send_sem=column_send.at[k * 7 + n],
+                recv_sem=column_recv.at[k * 7 + n],
+                device_id=across_column(dz, dc),
+                device_id_type=MESH,
+            )
+            copy.start()
+            column_copies.append(copy)
+        came[pz, c] = own[pz, c]
     first, second, third, relay, swaps = {}, {}, {}, {}, []
-    keep = []
-    for k in range(3):
-        local = pltpu.make_async_copy(owns[k], view(k, **here), local_sem.at[k])
-        local.start()
-        keep.append(local)
+    keep = {}
+    for k in (2, 0, 1):
+        if k < 2:
+            came = (came_g, came_u)[k]
+            for copy in column_copies[k * 7 : k * 7 + 7]:
+                copy.wait_recv()
+            for z in range(4):
+                for core in range(2):
+                    tall[:, pl.ds(20 * z + 10 * core, 10), :] = came[z, core].astype(F32)
+            owns[k][...] = tall[...].astype(BF)
+        keep[k] = pltpu.make_async_copy(owns[k], view(k, **here), local_sem.at[k])
+        keep[k].start()
         first[k] = [push(owns[k], view(k, **here), KINDS[k][0], by) for by in (1, 3, 2)]
     for k, (a, b, e) in enumerate(KINDS):
         keep[k].wait()
@@ -89,24 +119,27 @@
             swaps.append(push(part, part, "c", 1))
     for copy in swaps:
         copy.wait_recv()
-    for copy in started:
+    for copy in started + column_copies:
         copy.wait_send()
 
 
 COPIES = 3 * (3 + 3 + 2 + 2 + 5)
 
 
-def gather(owns):
-    shapes = [jax.ShapeDtypeStruct((2, 4, 4, 4, 2, *o.shape[1:]), o.dtype) for o in owns]
+def gather(own_g, own_u, own_d):
+    wide = jax.ShapeDtypeStruct((2, 4, 4, 80, 4096), BF)
     return pl.pallas_call(
         gather_kernel,
-        out_shape=shapes,
+        out_shape=[wide, wide, jax.ShapeDtypeStruct((2, 4, 4, 4, 2, 32, 1280), BF)],
         in_specs=[pl.BlockSpec(memory_space=pltpu.VMEM)] * 3,
         out_specs=[pl.BlockSpec(memory_space=pl.ANY)] * 3,
-        scratch_shapes=[pltpu.SemaphoreType.DMA((3,)), pltpu.SemaphoreType.DMA((COPIES,)), pltpu.SemaphoreType.DMA((COPIES,))],
+        scratch_shapes=[pltpu.VMEM((4, 2, 2, 10, 512), BF)] * 2
+        + [pltpu.VMEM((2, 80, 512), F32)]
+        + [pltpu.VMEM((2, 80, 512), BF)] * 2
+        + [pltpu.SemaphoreType.DMA((n,)) for n in (3, COPIES, COPIES, 14, 14)],
         compiler_params=pltpu.CompilerParams(collective_id=0, has_side_effects=True),
         name="gather",
-    )(*owns)
+    )(own_g, own_u, own_d)
 
 
 def place():
@@ -422,8 +455,8 @@
             own = lax.dynamic_slice(w, (0, me * rows, 0), (2, rows, w.shape[2])).astype(F32)
             new.append(adamw(own, m, v, g.astype(BF).astype(F32)))
         stacked = [[t[which] for t in new] for which in range(3)]
-        owns = [stacked[0][0].reshape(2, 320, 128), stacked[0][1].reshape(2, 320, 128), stacked[0][2]]
-        weights = [o.reshape(w.shape) for o, w in zip(gather(owns), (wg, wu, wd))]
+        cut = [t.reshape(2, 10, 2, 4, 512).transpose(3, 2, 0, 1, 4) for t in stacked[0][:2]]
+        weights = [o.reshape(w.shape) for o, w in zip(gather(*cut, stacked[0][2]), (wg, wu, wd))]
         return (*weights, *stacked[1], *stacked[2])
 
     rows = P(None, "dp", None)

time: 718 us -> 687 us (0.957)
  local copies, waits for them, and re-layouts: 90.1 us -> 52.7 us
  Pallas kernels: 359 us -> 368 us
    reshape x4, local copies, waits for them, and re-layouts: 64 us -> 1.73 us  [body(): t.reshape(2, 10, 2, 4, 512).transpose(3, 2, 0, 1, 4)]
    unnamed x36 -> x50, local copies, waits for them, and re-layouts: 25 us -> 49.9 us
    pallas_call x1, Pallas kernels: 142 us -> 151 us  [gather(): pl.pallas_call(gather_kernel, out_shape=[wide, wide, jax.ShapeDtypeStruct...]
where the time goes in v2:
time: 687 us; the launch traced here: 678 us
  Pallas kernels  368 us (54%)
  matrix products  238 us (35%)
  local copies, waits for them, and re-layouts  52.7 us (8%)
  other arithmetic  18.3 us (3%)
    pallas_call x2, Pallas kernels, scatter(): pl.pallas_call(functools.partial(scatter_kernel, len(beside)), out_shape=...  195 us
    pallas_call x1, Pallas kernels, gather(): pl.pallas_call(gather_kernel, out_shape=[wide, wide, jax.ShapeDtypeStruct...  151 us
    dot_general x4, matrix products, across(): lax.dot_general(a, w, (((1,), (1,)), ((), ())), preferred_element_type=F32)  87.3 us
    dot_general x3, matrix products, product_of(): lax.dot_general(a, b, (((0,), (0,)), ((), ())), preferred_element_type=F32)  55.4 us
    unnamed x50, local copies, waits for them, and re-layouts  49.9 us
    dot_general x2, matrix products, forward(): up = jnp.dot(a, wu, preferred_element_type=F32)  39.5 us
    dot_general x2, matrix products, forward(): gate = jnp.dot(a, wg, preferred_element_type=F32)  37.4 us
    pallas_call x1, Pallas kernels, column(): pl.pallas_call(column_kernel, out_shape=jax.ShapeDtypeStruct((2, n, 10, 1...  22.1 us

profile of v2, /device:TPU:1, one launch (start us, length us, event | category | flops | bytes accessed | tf_op | source)
XLA Modules:
  0.0 678.2 jit_solution(14603582445139807268)
XLA Ops:
  0.7 2.3 fusion.41
  3.0 3.8 fusion.42.rest_2_.rest_4_
  6.8 19.3 %fusion.24 = f32[1024,4096]{1,0:T(8,128)} fusion(bf16[2,1280,4096]{2,1,0:T(8,128)(2,1)} %param.13, bf16[1,1024,1280]{2,1,0:T(8,128)(2,1)} %param.11, f32[1024]{0:T(1024)S(1)} %add_rsqrt_fusion), kind=kOutput, calls=%fused_computation.35 | convolution fusion | flops 10741350400 | bytes 29888512 | tf_op jit(solution)/shard_map/dot_general | solution.py:401
  26.1 22.2 %multiply_convert_fusion.1 = (bf16[1024,4096]{1,0:T(8,128)(2,1)S(1)}, f32[1024,4096]{1,0:T(8,128)}) fusion(f32[1024,4096]{1,0:T(8,128)} %fusion.24, bf16[2,1280,4096]{2,1,0:T(8,128)(2,1)} %param.14, bf16[1,1024,1280]{2,1,0:T(8,128)(2,1)S(1)} %copy-done.2, f32[1024]{0:T(1024)S(1)} %add_rsqrt_fusion), kind=kOutput, calls=%fused_computation.13 | convolution fusion | flops 10766516224 | bytes 55054336 | tf_op jit(solution)/shard_map/dot_general | solution.py:402
  48.3 18.5 %fusion.45 = (f32[1024]{0:T(1024)S(1)}, bf16[1024,1280]{1,0:T(8,128)(2,1)S(1)}) fusion(bf16[1024,4096]{1,0:T(8,128)(2,1)S(1)} %get-tuple-element.59.rest_0_, bf16[2,4096,1280]{2,1,0:T(8,128)(2,1)} %param.15, bf16[1,1024,1280]{2,1,0:T(8,128)(2,1)S(1)} %copy-done.2), kind=kOutput, calls=%fused_computation.59 | convolution fusion | flops 10743970816 | bytes 24121344 | tf_op jit(solution)/shard_map/dot_general | solution.py:390
  66.9 18.1 %fusion.10 = f32[1024,4096]{1,0:T(8,128)} fusion(bf16[2,1280,4096]{2,1,0:T(8,128)(2,1)} %param.13, bf16[1024,1280]{1,0:T(8,128)(2,1)S(1)} %get-tuple-element.62, f32[1024]{0:T(1024)S(1)} %fusion.84), kind=kOutput, calls=%fused_computation.21 | convolution fusion | flops 10741350400 | bytes 29888512 | tf_op jit(solution)/shard_map/dot_general | solution.py:401
  85.0 17.3 %fusion.14 = f32[1024,4096]{1,0:T(8,128)} fusion(bf16[2,1280,4096]{2,1,0:T(8,128)(2,1)} %param.14, bf16[1024,1280]{1,0:T(8,128)(2,1)S(1)} %get-tuple-element.62, f32[1024]{0:T(1024)S(1)} %fusion.84), kind=kOutput, calls=%fused_computation.25 | convolution fusion | flops 10741350400 | bytes 29888512 | tf_op jit(solution)/shard_map/dot_general | solution.py:402
  102.3 20.5 %convolution_convert_fusion = bf16[4096,1280]{1,0:T(8,128)(2,1)} fusion(f32[1024,4096]{1,0:T(8,128)} %fusion.14, f32[1024,4096]{1,0:T(8,128)} %fusion.10, bf16[1,1024,1280]{2,1,0:T(8,128)(2,1)S(1)} %copy-done.4), kind=kOutput, calls=%fused_computation.16 | convolution fusion | flops 10767826944 | bytes 46661632 | tf_op jit(solution)/shard_map/dot_general | solution.py:413
  122.8 25.1 %fusion.2 = (bf16[1024,4096]{1,0:T(8,128)(2,1)}, bf16[1024,4096]{1,0:T(8,128)(2,1)}) fusion(f32[1024,4096]{1,0:T(8,128)} %fusion.10, f32[1024,4096]{1,0:T(8,128)} %fusion.14, bf16[2,4096,1280]{2,1,0:T(8,128)(2,1)} %param.15, bf16[1,1024,1280]{2,1,0:T(8,128)(2,1)S(1)} %copy-done.4), kind=kOutput, calls=%fused_computation.6 | convolution fusion | flops 10800332800 | bytes 63438848 | tf_op jit(solution)/shard_map/dot_general | solution.py:409
  147.9 17.7 %fusion.51 = bf16[1024,1280]{1,0:T(8,128)(2,1)} fusion(bf16[1024,4096]{1,0:T(8,128)(2,1)} %get-tuple-element.53, bf16[2,1280,4096]{2,1,0:T(8,128)(2,1)} %param.14), kind=kOutput, calls=%fused_computation.65 | convolution fusion | flops 10738728960 | bytes 21495808 | tf_op jit(solution)/shard_map/dot_general | solution.py:409
  165.7 18.3 %fusion.47 = (f32[1024]{0:T(1024)S(1)}, bf16[1024,1280]{1,0:T(8,128)(2,1)}) fusion(bf16[1024,1280]{1,0:T(8,128)(2,1)S(1)} %copy-done.6, bf16[1024,1280]{1,0:T(8,128)(2,1)} %fusion.51, bf16[1024,4096]{1,0:T(8,128)(2,1)} %get-tuple-element.54, bf16[2,1280,4096]{2,1,0:T(8,128)(2,1)} %param.13), kind=kOutput, calls=%fused_computation.61 | convolution fusion | flops 10749213696 | bytes 26742784 | tf_op jit(solution)/shard_map/dot_general | solution.py:409
  184.0 4.0 fusion.64.rest_1_
  188.0 26.1 %fusion.5 = (bf16[1024,4096]{1,0:T(8,128)(2,1)}, bf16[1024,4096]{1,0:T(8,128)(2,1)}) fusion(f32[1024,4096]{1,0:T(8,128)} %fusion.24, f32[1024,4096]{1,0:T(8,128)} %get-tuple-element.60, bf16[1024,1280]{1,0:T(8,128)(2,1)S(1)} %fusion.64.rest_1_, bf16[2,4096,1280]{2,1,0:T(8,128)(2,1)} %param.15), kind=kOutput, calls=%fused_computation.9 | convolution fusion | flops 10800332800 | bytes 63438848 | tf_op jit(solution)/shard_map/dot_general | solution.py:409
  214.1 17.9 %convolution_convert_fusion.2 = bf16[1280,4096]{1,0:T(8,128)(2,1)} fusion(bf16[1024,4096]{1,0:T(8,128)(2,1)} %get-tuple-element.54, bf16[1024,1280]{1,0:T(8,128)(2,1)} %copy-done.5, f32[1024]{0:T(1024)S(1)} %fusion.84), kind=kOutput, calls=%fused_computation.18 | convolution fusion | flops 10746593280 | bytes 21499904 | tf_op jit(solution)/shard_map/dot_general | solution.py:413
  232.0 17.1 %convolution_convert_fusion.1 = bf16[1280,4096]{1,0:T(8,128)(2,1)} fusion(bf16[1024,4096]{1,0:T(8,128)(2,1)} %get-tuple-element.53, bf16[1024,1280]{1,0:T(8,128)(2,1)S(1)} %copy-done.7, f32[1024]{0:T(1024)S(1)} %fusion.84), kind=kOutput, calls=%fused_computation.17 | convolution fusion | flops 10746593280 | bytes 21499904 | tf_op jit(solution)/shard_map/dot_general | solution.py:413
  249.0 103.9 %scatter1.1 = (f32[80,2048]{1,0:T(8,128)}, f32[80,2048]{1,0:T(8,128)}, f32[32,1280]{1,0:T(8,128)}, bf16[4096,1280]{1,0:T(8,128)(2,1)}, bf16[1280,4096]{1,0:T(8,128)(2,1)}, /*index=5*/bf16[1280,4096]{1,0:T(8,128)(2,1)}) custom-call(bf16[4,4,80,4096]{3,2,1,0:T(8,128)(2,1)} %bitcast.138, bf16[4,4,80,4096]{3,2,1,0:T(8,128)(2,1)} %bitcast.139, ...), custom_call_target="tpu_custom_call" | custom-call | tf_op jit(solution)/shard_map/scatter1/pallas_call | solution.py:309
  353.0 90.8 %scatter2.1 = (f32[80,2048]{1,0:T(8,128)}, f32[80,2048]{1,0:T(8,128)}, f32[32,1280]{1,0:T(8,128)}) custom-call(bf16[4,4,80,4096]{3,2,1,0:T(8,128)(2,1)} %bitcast.135, bf16[4,4,80,4096]{3,2,1,0:T(8,128)(2,1)} %bitcast.136, bf16[4,4,4,2,32,1280]{5,4,3,2,1,0:T(8,128)(2,1)} %bitcast.134), custom_call_target="tpu_custom_call" | custom-call | tf_op jit(solution)/shard_map/scatter2/pallas_call | solution.py:309
  443.8 1.2 copy.42
  445.0 1.2 copy.44
  446.2 1.0 convert_bitcast_fusion
  447.2 2.0 fusion.81
  449.2 1.2 copy.43
  451.6 1.3 convert_element_type.146.parts
  452.8 22.1 %column.1 = f32[2,4,10,16,128]{4,3,2,1,0:T(8,128)} custom-call(bf16[4,2,4,10,16,128]{5,4,3,2,1,0:T(8,128)(2,1)} %convert_element_type.146.parts, f32[4,10,16,128]{3,2,1,0:T(8,128)} %dynamic-slice_bitcast_fusion.kept), custom_call_target="tpu_custom_call" | custom-call | tf_op jit(solution)/shard_map/column/pallas_call | solution.py:370
  474.9 1.1 convert.30
  476.4 2.7 fusion.71
  484.8 150.8 %gather.1 = (bf16[2,4,4,80,4096]{4,3,2,1,0:T(8,128)(2,1)}, bf16[2,4,4,80,4096]{4,3,2,1,0:T(8,128)(2,1)}, bf16[2,4,4,4,2,32,1280]{6,5,4,3,2,1,0:T(8,128)(2,1)}) custom-call(bf16[4,2,2,10,512]{4,3,2,1,0:T(8,128)(2,1)} %bitcast.144, bf16[4,2,2,10,512]{4,3,2,1,0:T(8,128)(2,1)} %bitcast.145, bf16[2,32,1280]{2,1,0:T(8,128)(2,1)} %get-tuple-element.42.own_d), custom_call_target="tpu_custom_call" | custom-call | tf_op jit(solution)/shard_map/gather/pallas_call | solution.py:131
  635.7 21.1 %copy.72 = bf16[2,1280,4096]{2,1,0:T(8,128)(2,1)} copy(bf16[2,1280,4096]{2,1,0:T(8,128)(2,1)} %bitcast.133) | data formatting | bytes 41943040
  656.8 10.6 %copy.73 = bf16[2,1280,4096]{2,1,0:T(8,128)(2,1)} copy(bf16[2,1280,4096]{2,1,0:T(8,128)(2,1)S(1)} %bitcast.132) | data formatting | bytes 41943040
  667.4 1.6 slice-done.3
  669.0 1.2 slice-done.4
  670.2 7.5 %copy.74 = bf16[2,4096,1280]{2,1,0:T(8,128)(2,1)} copy(bf16[2,4096,1280]{2,1,0:T(8,128)(2,1)S(1)} %bitcast.131) | data formatting | bytes 41943040
  (61 shorter events, 7.1 us)
Async XLA Ops:
  6.8 19.3 %copy-start.2 = (bf16[1,1024,1280]{2,1,0:T(8,128)(2,1)S(1)}, bf16[1,1024,1280]{2,1,0:T(8,128)(2,1)}, u32[]{:S(2)}) copy-start(bf16[1,1024,1280]{2,1,0:T(8,128)(2,1)} %param.11) | copy-start | bytes 7864324
  48.3 18.5 %copy-start.3 = (bf16[1024,4096]{1,0:T(8,128)(2,1)}, bf16[1024,4096]{1,0:T(8,128)(2,1)S(1)}, u32[]{:S(2)}) copy-start(bf16[1024,4096]{1,0:T(8,128)(2,1)S(1)} %get-tuple-element.59.rest_0_) | copy-start | bytes 25165828
  66.8 18.2 %copy-start.5 = (bf16[1024,1280]{1,0:T(8,128)(2,1)}, bf16[1024,1280]{1,0:T(8,128)(2,1)S(1)}, u32[]{:S(2)}) copy-start(bf16[1024,1280]{1,0:T(8,128)(2,1)S(1)} %get-tuple-element.62) | copy-start | bytes 7864324
  66.8 18.2 %copy-start.11 = (f32[1024]{0:T(1024)}, f32[1024]{0:T(1024)S(1)}, u32[]{:S(2)}) copy-start(f32[1024]{0:T(1024)S(1)} %get-tuple-element.61) | copy-start | bytes 12292
  85.0 17.3 %copy-start.4 = (bf16[1,1024,1280]{2,1,0:T(8,128)(2,1)S(1)}, bf16[1,1024,1280]{2,1,0:T(8,128)(2,1)}, u32[]{:S(2)}) copy-start(bf16[1,1024,1280]{2,1,0:T(8,128)(2,1)} %param.12) | copy-start | bytes 7864324
  147.9 17.7 %copy-start.6 = (bf16[1024,1280]{1,0:T(8,128)(2,1)S(1)}, bf16[1024,1280]{1,0:T(8,128)(2,1)}, u32[]{:S(2)}) copy-start(bf16[1024,1280]{1,0:T(8,128)(2,1)} %copy-done.5) | copy-start | bytes 7864324
  165.7 18.3 %copy-start.12 = (f32[1024]{0:T(1024)S(1)}, f32[1024]{0:T(1024)}, u32[]{:S(2)}) copy-start(f32[1024]{0:T(1024)} %copy-done.11) | copy-start | bytes 12292
  188.0 26.1 %copy-start.1 = (bf16[1024,1280]{1,0:T(8,128)(2,1)}, bf16[1024,1280]{1,0:T(8,128)(2,1)S(1)}, u32[]{:S(2)}) copy-start(bf16[1024,1280]{1,0:T(8,128)(2,1)S(1)} %fusion.64.rest_1_) | copy-start | bytes 7864324
  214.1 17.9 %copy-start.7 = (bf16[1024,1280]{1,0:T(8,128)(2,1)S(1)}, bf16[1024,1280]{1,0:T(8,128)(2,1)}, u32[]{:S(2)}) copy-start(bf16[1024,1280]{1,0:T(8,128)(2,1)} %copy-done.5) | copy-start | bytes 7864324
  353.0 94.2 %copy-start.10 = (f32[2,32,1280]{2,1,0:T(8,128)S(1)}, f32[2,32,1280]{2,1,0:T(8,128)}, u32[]{:S(2)}) copy-start(f32[2,32,1280]{2,1,0:T(8,128)} %param.21) | copy-start | bytes 983044
  353.0 97.5 %copy-start.8 = (f32[80,2048]{1,0:T(8,128)S(1)}, f32[80,2048]{1,0:T(8,128)}, u32[]{:S(2)}) copy-start(f32[80,2048]{1,0:T(8,128)} %get-tuple-element.27) | copy-start | bytes 1966084
  450.4 26.0 %copy-start.9 = (f32[2,10,4096]{2,0,1:T(2,128)S(1)}, f32[2,10,4096]{2,0,1:T(2,128)}, u32[]{:S(2)}) copy-start(f32[2,10,4096]{2,0,1:T(2,128)} %param.19) | copy-start | bytes 983044
  635.7 21.2 %copy-start = (bf16[2,4,4,80,4096]{4,3,2,1,0:T(8,128)(2,1)S(1)}, bf16[2,4,4,80,4096]{4,3,2,1,0:T(8,128)(2,1)}, u32[]{:S(2)}) copy-start(bf16[2,4,4,80,4096]{4,3,2,1,0:T(8,128)(2,1)} %get-tuple-element.31) | copy-start | bytes 62914564
  635.7 31.8 %slice-start = ((s8[20971520]{0:T(1024)(128)(4,1)}), s8[4194304]{0:T(1024)(128)(4,1)S(1)}, s32[]{:S(2)}) async-start(s8[20971520]{0:T(1024)(128)(4,1)} %bitcast.129), calls=%async_computation | async-start | bytes 8388608
  635.7 31.8 %slice-start.1 = ((s8[20971520]{0:T(1024)(128)(4,1)}), s8[4194304]{0:T(1024)(128)(4,1)S(1)}, s32[]{:S(2)}) async-start(s8[20971520]{0:T(1024)(128)(4,1)} %bitcast.129), calls=%async_computation.1 | async-start | bytes 8388608
  635.7 31.8 %slice-start.2 = ((s8[20971520]{0:T(1024)(128)(4,1)}), s8[4194304]{0:T(1024)(128)(4,1)S(1)}, s32[]{:S(2)}) async-start(s8[20971520]{0:T(1024)(128)(4,1)} %bitcast.129), calls=%async_computation.2 | async-start | bytes 8388608
  656.8 12.2 %slice-start.3 = ((s8[20971520]{0:T(1024)(128)(4,1)}), s8[4194304]{0:T(1024)(128)(4,1)S(1)}, s32[]{:S(2)}) async-start(s8[20971520]{0:T(1024)(128)(4,1)} %bitcast.129), calls=%async_computation.3 | async-start | bytes 8388608
  656.8 13.4 %slice-start.4 = ((s8[20971520]{0:T(1024)(128)(4,1)}), s8[4194304]{0:T(1024)(128)(4,1)S(1)}, s32[]{:S(2)}) async-start(s8[20971520]{0:T(1024)(128)(4,1)} %bitcast.129), calls=%async_computation.4 | async-start | bytes 8388608
